TPU v7x, 32 devices: a whole 2x2x4 slice. The times are simulated.
32 devices in a mesh: terms: 32 (over z, y, x, core).
Axes of the slice: x: 2, y: 2, z: 4, core: 2. Of those that a mesh axis runs over, the one named last changes fastest.
Arguments:
- psi_init: float32 [512, 4, 4, 512], replicated
- left_env: bfloat16 [96, 512, 512], P('terms')
- op_pair: bfloat16 [96, 16, 16], P('terms')
- right_env: bfloat16 [96, 512, 512], P('terms')
Outputs:
- output 1: float32 [7, 512, 4, 4, 512], P(None, 'terms')
- output 2: float32 [6], replicated
- output 3: float32 [6], replicated
All inputs are finite; a program needn't handle non-finite values.
Results may differ from a plain program's by a relative error of at most 0.0168708.
Values are sent between devices in bfloat16 or wider.
A program may use at most 1 GiB of HBM per device.

v0:
```python
import jax
import jax.numpy as jnp
from jax import lax
from jax.sharding import PartitionSpec as P

KRYLOV_STEPS = 6


def solution(mesh):
    group_size = mesh.shape['terms']

    def local_run(psi_init, left_env, op_pair, right_env):
        bond_dim = psi_init.shape[0]
        phys_dim = psi_init.shape[1]
        pair_dim = phys_dim * phys_dim
        elem_count = bond_dim * pair_dim * bond_dim
        slab_rows = bond_dim // group_size
        row_start = lax.axis_index('terms') * slab_rows
        psi_full = psi_init.reshape(bond_dim, pair_dim, bond_dim)
        full_norm = jnp.sqrt(jnp.sum(psi_full * psi_full) / elem_count)
        vector = lax.dynamic_slice_in_dim(psi_full, row_start, slab_rows, 0) / full_norm
        vectors = [vector]
        alphas = []
        betas = []
        prev_vector = vector
        for step_idx in range(KRYLOV_STEPS):
            whole_vector = lax.all_gather(vector.astype(jnp.bfloat16), 'terms', axis=0, tiled=True)
            y_part = jnp.einsum('apc,kbc->kapb', whole_vector, right_env, preferred_element_type=jnp.float32).astype(jnp.bfloat16)
            z_part = jnp.einsum('kqp,kapb->kaqb', op_pair, y_part, preferred_element_type=jnp.float32).astype(jnp.bfloat16)
            partial_sigma = jnp.einsum('kax,kxqb->aqb', left_env, z_part, preferred_element_type=jnp.float32)
            sigma_slab = lax.psum_scatter(partial_sigma, 'terms', scatter_dimension=0, tiled=True)
            alpha_val = lax.psum(jnp.sum(sigma_slab * vector), 'terms') / elem_count
            residual = sigma_slab - alpha_val * vector
            if step_idx > 0:
                residual = residual - betas[-1] * prev_vector
            beta_val = jnp.sqrt(lax.psum(jnp.sum(residual * residual), 'terms') / elem_count)
            prev_vector = vector
            vector = residual / beta_val
            vectors.append(vector)
            alphas.append(alpha_val)
            betas.append(beta_val)
        krylov_vectors = jnp.stack(vectors).reshape(KRYLOV_STEPS + 1, slab_rows, phys_dim, phys_dim, bond_dim)
        return krylov_vectors, jnp.stack(alphas), jnp.stack(betas)

    return jax.shard_map(local_run, mesh=mesh, in_specs=(P(), P('terms'), P('terms'), P('terms')), out_specs=(P(None, 'terms'), P(), P()), check_vma=False)
```

profile of v0, /device:TPU:0, one launch (start us, length us, event | category | flops | bytes accessed | tf_op | source)
XLA Modules:
  0.0 2756.9 jit_solution(6531221097853824465)
XLA Ops:
  7.2 19.5 reshape.24
  26.7 10.9 multiply_reduce_fusion
  38.3 1.8 fusion.83
  40.2 79.7 %all-gather.7.cloned.1.call-done = bf16[512,16,512]{2,1,0:T(8,128)(2,1)} async-done(((bf16[16,16,512]{2,1,0:T(8,128)(2,1)}), bf16[512,16,512]{2,1,0:T(8,128)(2,1)}) %all-gather.7.cloned.1.call-update) | async-done | bytes 8388624 | tf_op jit(solution)/shard_map/all_gather | solution.py:27
  119.9 20.5 convert_bitcast_fusion.11
  140.4 20.5 convert_bitcast_fusion.10
  160.9 42.4 %fusion.36 = f32[512,16,512]{0,2,1:T(8,128)} fusion(bf16[3,512,16,512]{3,2,1,0:T(8,128)(2,1)} %convert_bitcast_fusion.10, bf16[3,512,512]{2,1,0:T(8,128)(2,1)} %param.5), kind=kOutput, calls=%fused_computation.37 | convolution fusion | flops 12884901888 | bytes 43515904 | tf_op jit(solution)/shard_map/kax,kxqb->aqb/dot_general | solution.py:30
  203.3 20.2 copy.23
  223.6 181.8 %reduce-scatter.7.cloned.1.call-done = f32[16,16,512]{2,1,0:T(8,128)} async-done(((f32[512,16,512]{2,1,0:T(8,128)}), f32[16,16,512]{2,1,0:T(8,128)}) %reduce-scatter.7.cloned.1.call-update) | async-done | bytes 524304 | tf_op jit(solution)/shard_map/reduce_scatter | solution.py:31
  405.4 1.8 multiply_reduce_fusion.12
  407.2 42.5 %psum.84 = f32[]{:T(128)} all-reduce(f32[]{:T(128)} %multiply_reduce_fusion.12), channel_id=1, replica_groups=mesh['terms'=32] {'terms'}, use_global_device_ids=true, to_apply=%region_3.0 | all-reduce | flops 1 | bytes 8 | tf_op jit(solution)/shard_map/psum | solution.py:32
  450.4 1.8 multiply_reduce_fusion.11
  452.2 38.7 %psum.85 = f32[]{:T(128)} all-reduce(f32[]{:T(128)} %multiply_reduce_fusion.11), channel_id=1, replica_groups=mesh['terms'=32] {'terms'}, use_global_device_ids=true, to_apply=%region_5.0 | all-reduce | flops 1 | bytes 8 | tf_op jit(solution)/shard_map/psum | solution.py:36
  491.6 1.9 fusion.82
  493.5 78.1 %all-gather.9.cloned.1.call-done = bf16[512,16,512]{2,1,0:T(8,128)(2,1)} async-done(((bf16[16,16,512]{2,1,0:T(8,128)(2,1)}), bf16[512,16,512]{2,1,0:T(8,128)(2,1)}) %all-gather.9.cloned.1.call-update) | async-done | bytes 8388624 | tf_op jit(solution)/shard_map/all_gather | solution.py:27
  571.6 20.5 convert_bitcast_fusion.9
  592.2 20.5 convert_bitcast_fusion.8
  612.6 42.4 %fusion.39 = f32[512,16,512]{0,2,1:T(8,128)} fusion(bf16[3,512,16,512]{3,2,1,0:T(8,128)(2,1)} %convert_bitcast_fusion.8, bf16[3,512,512]{2,1,0:T(8,128)(2,1)} %param.5), kind=kOutput, calls=%fused_computation.38 | convolution fusion | flops 12884901888 | bytes 43515904 | tf_op jit(solution)/shard_map/kax,kxqb->aqb/dot_general | solution.py:30
  655.0 20.2 copy.26
  675.3 181.8 %reduce-scatter.9.cloned.1.call-done = f32[16,16,512]{2,1,0:T(8,128)} async-done(((f32[512,16,512]{2,1,0:T(8,128)}), f32[16,16,512]{2,1,0:T(8,128)}) %reduce-scatter.9.cloned.1.call-update) | async-done | bytes 524304 | tf_op jit(solution)/shard_map/reduce_scatter | solution.py:31
  857.2 1.8 multiply_reduce_fusion.10
  859.0 42.5 %psum.86 = f32[]{:T(128)} all-reduce(f32[]{:T(128)} %multiply_reduce_fusion.10), channel_id=1, replica_groups=mesh['terms'=32] {'terms'}, use_global_device_ids=true, to_apply=%region_8.0 | all-reduce | flops 1 | bytes 8 | tf_op jit(solution)/shard_map/psum | solution.py:32
  902.1 1.8 multiply_reduce_fusion.9
  903.9 38.7 %psum.87 = f32[]{:T(128)} all-reduce(f32[]{:T(128)} %get-tuple-element.19), channel_id=1, replica_groups=mesh['terms'=32] {'terms'}, use_global_device_ids=true, to_apply=%region_10.0 | all-reduce | flops 1 | bytes 8 | tf_op jit(solution)/shard_map/psum | solution.py:36
  944.2 78.1 %all-gather.11.cloned.1.call-done = bf16[512,16,512]{2,1,0:T(8,128)(2,1)} async-done(((bf16[16,16,512]{2,1,0:T(8,128)(2,1)}), bf16[512,16,512]{2,1,0:T(8,128)(2,1)}) %all-gather.11.cloned.1.call-update) | async-done | bytes 8388624 | tf_op jit(solution)/shard_map/all_gather | solution.py:27
  1022.3 20.5 convert_bitcast_fusion.7
  1042.9 20.5 convert_bitcast_fusion.6
  1063.3 42.4 %fusion.42 = f32[512,16,512]{0,2,1:T(8,128)} fusion(bf16[3,512,16,512]{3,2,1,0:T(8,128)(2,1)} %convert_bitcast_fusion.6, bf16[3,512,512]{2,1,0:T(8,128)(2,1)} %param.5), kind=kOutput, calls=%fused_computation.39 | convolution fusion | flops 12884901888 | bytes 43515904 | tf_op jit(solution)/shard_map/kax,kxqb->aqb/dot_general | solution.py:30
  1105.7 20.2 copy.29
  1126.0 181.8 %reduce-scatter.11.cloned.1.call-done = f32[16,16,512]{2,1,0:T(8,128)} async-done(((f32[512,16,512]{2,1,0:T(8,128)}), f32[16,16,512]{2,1,0:T(8,128)}) %reduce-scatter.11.cloned.1.call-update) | async-done | bytes 524304 | tf_op jit(solution)/shard_map/reduce_scatter | solution.py:31
  1307.9 1.8 multiply_reduce_fusion.8
  1309.7 42.5 %psum.88 = f32[]{:T(128)} all-reduce(f32[]{:T(128)} %multiply_reduce_fusion.8), channel_id=1, replica_groups=mesh['terms'=32] {'terms'}, use_global_device_ids=true, to_apply=%region_13.0 | all-reduce | flops 1 | bytes 8 | tf_op jit(solution)/shard_map/psum | solution.py:32
  1352.9 1.8 multiply_reduce_fusion.7
  1354.7 38.7 %psum.89 = f32[]{:T(128)} all-reduce(f32[]{:T(128)} %get-tuple-element.15), channel_id=1, replica_groups=mesh['terms'=32] {'terms'}, use_global_device_ids=true, to_apply=%region_15.0 | all-reduce | flops 1 | bytes 8 | tf_op jit(solution)/shard_map/psum | solution.py:36
  1394.9 78.1 %all-gather.13.cloned.1.call-done = bf16[512,16,512]{2,1,0:T(8,128)(2,1)} async-done(((bf16[16,16,512]{2,1,0:T(8,128)(2,1)}), bf16[512,16,512]{2,1,0:T(8,128)(2,1)}) %all-gather.13.cloned.1.call-update) | async-done | bytes 8388624 | tf_op jit(solution)/shard_map/all_gather | solution.py:27
  1473.1 20.5 convert_bitcast_fusion.5
  1493.6 20.5 convert_bitcast_fusion.4
  1514.1 42.4 %fusion.45 = f32[512,16,512]{0,2,1:T(8,128)} fusion(bf16[3,512,16,512]{3,2,1,0:T(8,128)(2,1)} %convert_bitcast_fusion.4, bf16[3,512,512]{2,1,0:T(8,128)(2,1)} %param.5), kind=kOutput, calls=%fused_computation.40 | convolution fusion | flops 12884901888 | bytes 43515904 | tf_op jit(solution)/shard_map/kax,kxqb->aqb/dot_general | solution.py:30
  1556.4 20.2 copy.32
  1576.8 181.8 %reduce-scatter.13.cloned.1.call-done = f32[16,16,512]{2,1,0:T(8,128)} async-done(((f32[512,16,512]{2,1,0:T(8,128)}), f32[16,16,512]{2,1,0:T(8,128)}) %reduce-scatter.13.cloned.1.call-update) | async-done | bytes 524304 | tf_op jit(solution)/shard_map/reduce_scatter | solution.py:31
  1758.6 1.8 multiply_reduce_fusion.6
  1760.4 42.5 %psum.90 = f32[]{:T(128)} all-reduce(f32[]{:T(128)} %multiply_reduce_fusion.6), channel_id=1, replica_groups=mesh['terms'=32] {'terms'}, use_global_device_ids=true, to_apply=%region_18.0 | all-reduce | flops 1 | bytes 8 | tf_op jit(solution)/shard_map/psum | solution.py:32
  1803.6 1.8 multiply_reduce_fusion.5
  1805.4 38.7 %psum.91 = f32[]{:T(128)} all-reduce(f32[]{:T(128)} %get-tuple-element.11), channel_id=1, replica_groups=mesh['terms'=32] {'terms'}, use_global_device_ids=true, to_apply=%region_20.0 | all-reduce | flops 1 | bytes 8 | tf_op jit(solution)/shard_map/psum | solution.py:36
  1845.7 78.1 %all-gather.15.cloned.1.call-done = bf16[512,16,512]{2,1,0:T(8,128)(2,1)} async-done(((bf16[16,16,512]{2,1,0:T(8,128)(2,1)}), bf16[512,16,512]{2,1,0:T(8,128)(2,1)}) %all-gather.15.cloned.1.call-update) | async-done | bytes 8388624 | tf_op jit(solution)/shard_map/all_gather | solution.py:27
  1923.8 20.5 convert_bitcast_fusion.3
  1944.3 20.5 convert_bitcast_fusion.2
  1964.8 42.4 %fusion.48 = f32[512,16,512]{0,2,1:T(8,128)} fusion(bf16[3,512,16,512]{3,2,1,0:T(8,128)(2,1)} %convert_bitcast_fusion.2, bf16[3,512,512]{2,1,0:T(8,128)(2,1)} %param.5), kind=kOutput, calls=%fused_computation.41 | convolution fusion | flops 12884901888 | bytes 43515904 | tf_op jit(solution)/shard_map/kax,kxqb->aqb/dot_general | solution.py:30
  2007.2 20.2 copy.35
  2027.5 181.8 %reduce-scatter.15.cloned.1.call-done = f32[16,16,512]{2,1,0:T(8,128)} async-done(((f32[512,16,512]{2,1,0:T(8,128)}), f32[16,16,512]{2,1,0:T(8,128)}) %reduce-scatter.15.cloned.1.call-update) | async-done | bytes 524304 | tf_op jit(solution)/shard_map/reduce_scatter | solution.py:31
  2211.1 42.5 %psum.92 = f32[]{:T(128)} all-reduce(f32[]{:T(128)} %multiply_reduce_fusion.4), channel_id=1, replica_groups=mesh['terms'=32] {'terms'}, use_global_device_ids=true, to_apply=%region_23.0 | all-reduce | flops 1 | bytes 8 | tf_op jit(solution)/shard_map/psum | solution.py:32
  2254.3 1.8 multiply_reduce_fusion.3
  2256.1 38.7 %psum.93 = f32[]{:T(128)} all-reduce(f32[]{:T(128)} %get-tuple-element.7), channel_id=1, replica_groups=mesh['terms'=32] {'terms'}, use_global_device_ids=true, to_apply=%region_25.0 | all-reduce | flops 1 | bytes 8 | tf_op jit(solution)/shard_map/psum | solution.py:36
  2296.6 78.1 %all-gather.17.cloned.1.call-done = bf16[512,16,512]{2,1,0:T(8,128)(2,1)} async-done(((bf16[16,16,512]{2,1,0:T(8,128)(2,1)}), bf16[512,16,512]{2,1,0:T(8,128)(2,1)}) %all-gather.17.cloned.1.call-update) | async-done | bytes 8388624 | tf_op jit(solution)/shard_map/all_gather | solution.py:27
  2374.7 20.5 convert_bitcast_fusion.1
  2395.2 20.6 convert_bitcast_fusion
  2415.8 42.0 %fusion.51 = f32[512,16,512]{0,2,1:T(8,128)} fusion(bf16[3,512,16,512]{3,2,1,0:T(8,128)(2,1)} %convert_bitcast_fusion, bf16[3,512,512]{2,1,0:T(8,128)(2,1)S(1)} %copy-done.10), kind=kOutput, calls=%fused_computation.42 | convolution fusion | flops 12884901888 | bytes 43515904 | tf_op jit(solution)/shard_map/kax,kxqb->aqb/dot_general | solution.py:30
  2457.8 20.3 copy.38
  2480.1 1.9 constant_dynamic-update-slice_fusion.6
  2489.2 170.8 %reduce-scatter.17.cloned.1.call-done = f32[16,16,512]{2,1,0:T(8,128)} async-done(((f32[512,16,512]{2,1,0:T(8,128)}), f32[16,16,512]{2,1,0:T(8,128)}) %reduce-scatter.17.cloned.1.call-update) | async-done | bytes 524304 | tf_op jit(solution)/shard_map/reduce_scatter | solution.py:31
  2660.0 1.9 multiply_reduce_fusion.2
  2662.8 42.5 %psum.94 = f32[]{:T(128)} all-reduce(f32[]{:T(128)} %multiply_reduce_fusion.2), channel_id=1, replica_groups=mesh['terms'=32] {'terms'}, use_global_device_ids=true, to_apply=%region_28.0 | all-reduce | flops 1 | bytes 8 | tf_op jit(solution)/shard_map/psum | solution.py:32
  2706.0 2.2 multiply_reduce_fusion.1
  2708.2 38.7 %psum.95 = f32[]{:T(128)} all-reduce(f32[]{:T(128)} %get-tuple-element.3), channel_id=1, replica_groups=mesh['terms'=32] {'terms'}, use_global_device_ids=true, to_apply=%region_30.0 | all-reduce | flops 1 | bytes 8 | tf_op jit(solution)/shard_map/psum | solution.py:36
  (67 shorter events, 18.1 us)
Async XLA Ops:
  7.2 112.7 %copy-start = (bf16[3,512,512]{2,1,0:T(8,128)(2,1)S(1)}, bf16[3,512,512]{2,1,0:T(8,128)(2,1)}, u32[]{:S(2)}) copy-start(bf16[3,512,512]{2,1,0:T(8,128)(2,1)} %param.7) | copy-start | bytes 4718596
  7.2 112.7 %all-gather.7.cloned.1.call-start = ((), (), s32[]{:S(2)}) async-start(), calls=%async_computation.6 | async-start | bytes 8650752 | tf_op jit(solution)/shard_map/all_gather | solution.py:27
  40.1 862.0 %copy-start.1 = (f32[16,16,512]{2,1,0:T(8,128)}, f32[16,16,512]{2,1,0:T(8,128)S(1)}, u32[]{:S(2)}) copy-start(f32[16,16,512]{2,1,0:T(8,128)S(1)} %get-tuple-element.24) | copy-start | bytes 1572868
  40.2 100.3 %copy-start.9 = (bf16[3,16,16]{2,1,0:T(8,128)(2,1)S(1)}, bf16[3,16,16]{2,1,0:T(8,128)(2,1)}, u32[]{:S(2)}) copy-start(bf16[3,16,16]{2,1,0:T(8,128)(2,1)} %param.6) | copy-start | bytes 4612
  40.2 365.2 %reduce-scatter.7.cloned.1.call-start = ((), (), s32[]{:S(2)}) async-start(), calls=%async_computation.7 | async-start | bytes 17301504 | tf_op jit(solution)/shard_map/reduce_scatter | solution.py:31
  223.5 348.1 %all-gather.9.cloned.1.call-start = ((), (), s32[]{:S(2)}) async-start(), calls=%async_computation.8 | async-start | bytes 8650752 | tf_op jit(solution)/shard_map/all_gather | solution.py:27
  493.4 859.4 %copy-start.3 = (f32[16,16,512]{2,1,0:T(8,128)}, f32[16,16,512]{2,1,0:T(8,128)S(1)}, u32[]{:S(2)}) copy-start(f32[16,16,512]{2,1,0:T(8,128)S(1)} %get-tuple-element.22) | copy-start | bytes 1572868
  493.4 363.7 %reduce-scatter.9.cloned.1.call-start = ((), (), s32[]{:S(2)}) async-start(), calls=%async_computation.9 | async-start | bytes 17301504 | tf_op jit(solution)/shard_map/reduce_scatter | solution.py:31
  675.3 347.1 %all-gather.11.cloned.1.call-start = ((), (), s32[]{:S(2)}) async-start(), calls=%async_computation.10 | async-start | bytes 8650752 | tf_op jit(solution)/shard_map/all_gather | solution.py:27
  944.1 859.4 %copy-start.5 = (f32[16,16,512]{2,1,0:T(8,128)}, f32[16,16,512]{2,1,0:T(8,128)S(1)}, u32[]{:S(2)}) copy-start(f32[16,16,512]{2,1,0:T(8,128)S(1)} %get-tuple-element.18) | copy-start | bytes 1572868
  944.2 363.7 %reduce-scatter.11.cloned.1.call-start = ((), (), s32[]{:S(2)}) async-start(), calls=%async_computation.11 | async-start | bytes 17301504 | tf_op jit(solution)/shard_map/reduce_scatter | solution.py:31
  1126.0 347.1 %all-gather.13.cloned.1.call-start = ((), (), s32[]{:S(2)}) async-start(), calls=%async_computation.12 | async-start | bytes 8650752 | tf_op jit(solution)/shard_map/all_gather | solution.py:27
  1394.9 859.4 %copy-start.7 = (f32[16,16,512]{2,1,0:T(8,128)}, f32[16,16,512]{2,1,0:T(8,128)S(1)}, u32[]{:S(2)}) copy-start(f32[16,16,512]{2,1,0:T(8,128)S(1)} %get-tuple-element.14) | copy-start | bytes 1572868
  1394.9 363.7 %reduce-scatter.13.cloned.1.call-start = ((), (), s32[]{:S(2)}) async-start(), calls=%async_computation.13 | async-start | bytes 17301504 | tf_op jit(solution)/shard_map/reduce_scatter | solution.py:31
  1576.7 347.1 %all-gather.15.cloned.1.call-start = ((), (), s32[]{:S(2)}) async-start(), calls=%async_computation.14 | async-start | bytes 8650752 | tf_op jit(solution)/shard_map/all_gather | solution.py:27
  1845.6 408.7 %copy-start.8 = (f32[16,16,512]{2,1,0:T(8,128)}, f32[16,16,512]{2,1,0:T(8,128)S(1)}, u32[]{:S(2)}) copy-start(f32[16,16,512]{2,1,0:T(8,128)S(1)} %get-tuple-element.10) | copy-start | bytes 1572868
  1845.6 363.7 %reduce-scatter.15.cloned.1.call-start = ((), (), s32[]{:S(2)}) async-start(), calls=%async_computation.15 | async-start | bytes 17301504 | tf_op jit(solution)/shard_map/reduce_scatter | solution.py:31
  2027.4 347.3 %all-gather.17.cloned.1.call-start = ((), (), s32[]{:S(2)}) async-start(), calls=%async_computation.16 | async-start | bytes 8650752 | tf_op jit(solution)/shard_map/all_gather | solution.py:27
  2296.5 363.5 %reduce-scatter.17.cloned.1.call-start = ((), (), s32[]{:S(2)}) async-start(), calls=%async_computation.17 | async-start | bytes 17301504 | tf_op jit(solution)/shard_map/reduce_scatter | solution.py:31
  2395.2 20.6 copy-start.10
  2478.1 1.0 copy-start.2
  2478.1 3.9 copy-start.4
  2478.1 4.9 copy-start.6
Sparse Core Ops, SparseCore 0:
  40.3 79.5 all-gather.6
  223.7 181.6 reduce-scatter.6
  493.6 78.0 all-gather.8
  675.4 181.7 reduce-scatter.8
  944.3 78.0 all-gather.10
  1126.1 181.7 reduce-scatter.10
  1395.0 78.0 all-gather.12
  1576.8 181.7 reduce-scatter.12
  1845.7 78.0 all-gather.14
  2027.6 181.7 reduce-scatter.14
  2296.7 78.0 all-gather.16
  2478.3 181.7 reduce-scatter.16
where the time goes:
time: 2770 us; the launch traced here: 2760 us
  waiting for transfers between devices  1550 us (56%)
  matrix products  500 us (18%)
  blocking collectives  487 us (18%)
  local copies, waits for them, and re-layouts  155 us (6%)
  other arithmetic  40 us (1%)
    reduce_scatter x6, waiting for transfers between devices, local_run(): lax.psum_scatter(partial_sigma, 'terms', scatter_dimension=0, tiled=True)  1080 us
    all_gather x6, waiting for transfers between devices, local_run(): lax.all_gather(vector.astype(jnp.bfloat16), 'terms', axis=0, tiled=True)  470 us
    psum x6, blocking collectives, local_run(): alpha_val = lax.psum(jnp.sum(sigma_slab * vector), 'terms') / elem_count  255 us
    dot_general x6, matrix products, local_run(): jnp.einsum('kax,kxqb->aqb', left_env, z_part, preferred_element_type=jnp....  254 us
    psum x6, blocking collectives, local_run(): lax.psum(jnp.sum(residual * residual), 'terms') / elem_count  232 us
    dot_general x6, matrix products, local_run(): jnp.einsum('apc,kbc->kapb', whole_vector, right_env, preferred_element_ty...  123 us
    dot_general x6, matrix products, local_run(): jnp.einsum('kqp,kapb->kaqb', op_pair, y_part, preferred_element_type=jnp....  123 us
    dot_general x6, local copies, waits for them, and re-layouts, local_run(): jnp.einsum('kax,kxqb->aqb', left_env, z_part, preferred_element_type=jnp....  121 us
  transfers between devices with their start and end apart: 12, of which 12 were waited for; matrix products, arithmetic and copies ran while one was open for 0% of the time, Pallas kernels for 0%

commit v1 on v0

v1 whole, which is shorter than its diff:
```python
import functools

import jax
import jax.numpy as jnp
from jax import lax
from jax.experimental import pallas as pl
from jax.experimental.pallas import tpu as pltpu
from jax.sharding import PartitionSpec as P

KRYLOV_STEPS = 6
MESH = pl.DeviceIdType.MESH
NDEV = 32
NT = 96
NC = 4
GP = 4
GR = 16


def coords(me):
    z = me // 8
    return z // 2, lax.rem(z, 2), lax.rem(me // 4, 2), lax.rem(me // 2, 2), lax.rem(me, 2)


def dev_id(zh, zl, y, x, c):
    return zh * 16 + zl * 8 + y * 4 + x * 2 + c


def kernel(elem_count, vb0_ref, lh_ref, kr_ref, rr_ref, v0_ref, out_ref, alpha_ref, beta_ref,
           vbuf, vsend, xs, sacc, rsr, vs, arr, bsc,
           in_sem, out_sem, rs_send, rs_recv, ar_send, ar_recv, aa_send, aa_recv, ag_send, ag_recv):
    f32, bf16 = jnp.float32, jnp.bfloat16
    me = lax.axis_index('terms')
    zh, zl, y, x, c = coords(me)
    role = 2 * zl + x
    unit = 4 * zh + 2 * y + c
    inv_n = 1.0 / elem_count
    rs_dev = [dev_id(zh, zl, y, 1 - x, c), dev_id(zh, 1 - zl, y, x, c), dev_id(zh, 1 - zl, y, 1 - x, c)]
    rs_role = [2 * zl + (1 - x), 2 * (1 - zl) + x, 2 * (1 - zl) + (1 - x), role]
    dev_z = dev_id(1 - zh, zl, y, x, c)
    dev_y = dev_id(zh, zl, 1 - y, x, c)
    dev_c = dev_id(zh, zl, y, x, 1 - c)
    own_rows = pl.ds(pl.multiple_of(role * 16, 16), 16)
    ppc = 8 // NC

    def aa_copy(ch, i):
        pps = pl.ds(ch * ppc, ppc)
        return pltpu.make_async_remote_copy(
            src_ref=vsend.at[rs_role[i], pps], dst_ref=vbuf.at[unit, pps, own_rows],
            send_sem=aa_send.at[ch, i], recv_sem=aa_recv.at[ch, i], device_id=(rs_dev[i],), device_id_type=MESH)

    def ag_copy(ch, slot, u, dev):
        pps = pl.ds(ch * ppc, ppc)
        return pltpu.make_async_remote_copy(
            src_ref=vbuf.at[u, pps], dst_ref=vbuf.at[u, pps],
            send_sem=ag_send.at[ch, slot], recv_sem=ag_recv.at[ch, u], device_id=(dev,), device_id_type=MESH)

    unit_z = 4 * (1 - zh) + 2 * y + c
    unit_y = 4 * zh + 2 * (1 - y) + c
    unit_zy = 4 * (1 - zh) + 2 * (1 - y) + c
    sends = [(0, unit, dev_z), (1, unit, dev_y), (2, unit_z, dev_y),
             (3, unit, dev_c), (4, unit_z, dev_c), (5, unit_y, dev_c), (6, unit_zy, dev_c)]

    def start(ch, slots):
        for s in slots:
            ag_copy(ch, *sends[s]).start()

    def recv(ch, u):
        ag_copy(ch, 0, u, dev_c).wait_recv()

    def stage_a(ch):
        for i in range(3):
            aa_copy(ch, i).wait_recv()
        start(ch, (0, 1, 3))

    def stage_z(ch):
        recv(ch, unit_z)
        start(ch, (2, 4))

    def stage_y(ch):
        recv(ch, unit_y)
        start(ch, (5,))
        recv(ch, unit_zy)
        start(ch, (6,))

    def stage_c(ch):
        for a in range(2):
            for b in range(2):
                recv(ch, 4 * a + 2 * b + (1 - c))

    def left_chunk(ch):
        def body(i, _):
            pp = ch * ppc + i // 4
            ac = lax.rem(i, 4)
            slab = jnp.where(ac == 0, rs_role[0], jnp.where(ac == 1, rs_role[1], jnp.where(ac == 2, rs_role[2], role)))
            rhs = vbuf[:, pp].reshape(512, 256)
            res = jnp.dot(lh_ref[slab], rhs, preferred_element_type=f32).astype(bf16).reshape(NT, 16, 256)
            ap = ac // 2

            @pl.when(lax.rem(ac, 2) == 0)
            def _():
                xs[ap, :, 2 * pp, :, 0:128] = res[:, :, 0:128]
                xs[ap, :, 2 * pp + 1, :, 0:128] = res[:, :, 128:256]

            @pl.when(lax.rem(ac, 2) == 1)
            def _():
                xs[ap, :, 2 * pp, :, 128:256] = res[:, :, 0:128]
                xs[ap, :, 2 * pp + 1, :, 128:256] = res[:, :, 128:256]
            return 0
        lax.fori_loop(0, ppc * 4, body, 0)

    def pair_phase(ap):
        def body(i, _):
            for g in range(GP):
                k = i * GP + g
                zval = jnp.dot(kr_ref[k], xs[ap, k].reshape(256, 256), preferred_element_type=f32).astype(bf16)
                xs[ap, k] = zval.reshape(16, 16, 256)
            return 0
        lax.fori_loop(0, NT // GP, body, 0)

    def right_phase(ap, h, dst):
        def piece(k0):
            lhs = jnp.concatenate([xs[ap, k0 + g].reshape(256, 256)[:, h * 128:(h + 1) * 128] for g in range(GR)], axis=1)
            rhs = rr_ref[pl.ds(k0, GR)].reshape(GR * 128, 512)
            return jnp.dot(lhs, rhs, preferred_element_type=f32).reshape(16, 16, 512)
        sacc[dst] = jnp.zeros((16, 16, 512), f32)

        def body(i, _):
            sacc[dst] += piece(i * GR)
            return 0
        lax.fori_loop(0, NT // GR, body, 0)

    def rs_copy(i):
        return pltpu.make_async_remote_copy(
            src_ref=sacc.at[i], dst_ref=rsr.at[i], send_sem=rs_send.at[i], recv_sem=rs_recv.at[i],
            device_id=(rs_dev[i],), device_id_type=MESH)

    def total(val):
        return jnp.sum(jnp.sum(val, axis=0, keepdims=True), axis=1, keepdims=True)

    def out_copy(slot, j):
        return pltpu.make_async_copy(vs.at[slot], out_ref.at[j], out_sem)

    loads = [pltpu.make_async_copy(v0_ref, vs.at[0], in_sem.at[0]), pltpu.make_async_copy(vb0_ref, vbuf, in_sem.at[1])]
    for cp in loads:
        cp.start()
    vs[2] = jnp.zeros((16, 16, 512), f32)
    bsc[...] = jnp.zeros((8, 128), f32)
    for cp in loads:
        cp.wait()
    out_copy(0, 0).start()

    def step(j, _):
        cur = lax.rem(j, 3)
        nxt = lax.rem(j + 1, 3)
        prv = lax.rem(j + 2, 3)
        par = lax.rem(j, 2)

        @pl.when(j > 0)
        def _():
            for t in range(NC + 2):
                if t < NC:
                    stage_a(t)
                if 0 <= t - 1 < NC:
                    stage_z(t - 1)
                if 0 <= t - 2 < NC:
                    stage_y(t - 2)

        for ch in range(NC):
            @pl.when(j > 0)
            def _():
                stage_c(ch)
            left_chunk(ch)

        @pl.when(j > 0)
        def _():
            for ch in range(NC):
                for i in range(3):
                    aa_copy(ch, i).wait_send()
                for s in sends:
                    ag_copy(ch, *s).wait_send()

        pair_phase(0)
        right_phase(0, 0, 0)
        rs_copy(0).start()
        right_phase(0, 1, 1)
        rs_copy(1).start()
        pair_phase(1)
        right_phase(1, 0, 2)
        rs_copy(2).start()
        right_phase(1, 1, 3)
        out_copy(cur, j).wait()
        for i in range(3):
            rs_copy(i).wait()

        beta_prev = bsc[0:1, 0:1]

        def pass1(p, acc):
            s1, sb, vv = acc
            w = ((sacc[3, p] + rsr[0, p]) + (rsr[1, p] + rsr[2, p]))
            v = vs[cur, p]
            sacc[3, p] = w
            return s1 + w * v, sb + (w - beta_prev * vs[prv, p]) * v, vv + v * v
        zero = jnp.zeros((16, 512), f32)
        s1, sb, vv = lax.fori_loop(0, 16, pass1, (zero, zero, zero))
        s1, sb, vv = total(s1), total(sb), total(vv)
        a_loc = jnp.where(vv > 1e-6, sb / jnp.where(vv > 1e-6, vv, 1.0), 0.0)

        def pass2(p, acc):
            uu, uv = acc
            v = vs[cur, p]
            u = sacc[3, p] - beta_prev * vs[prv, p] - a_loc * v
            return uu + u * u, uv + u * v
        uu, uv = lax.fori_loop(0, 16, pass2, (zero, zero))
        uu, uv = total(uu), total(uv)
        row = lax.broadcasted_iota(jnp.int32, (8, 128), 0)
        msg = jnp.where(row == 0, s1, jnp.where(row == 1, a_loc, jnp.where(row == 2, uu, jnp.where(row == 3, uv, vv))))
        arr[par, me] = msg

        def ar_copy(i):
            return pltpu.make_async_remote_copy(
                src_ref=arr.at[par, me], dst_ref=arr.at[par, me], send_sem=ar_send, recv_sem=ar_recv,
                device_id=(lax.rem(me + i, NDEV),), device_id_type=MESH)

        def send_msg(i, _):
            ar_copy(i).start()
            return 0
        lax.fori_loop(1, NDEV, send_msg, 0)
        pltpu.make_async_copy(arr.at[par, pl.ds(0, NDEV - 1)], arr.at[par, pl.ds(0, NDEV - 1)], ar_recv).wait()
        pltpu.make_async_copy(arr.at[par, pl.ds(0, NDEV - 1)], arr.at[par, pl.ds(0, NDEV - 1)], ar_send).wait()
        alpha = jnp.sum(arr[par, :, 0], axis=0, keepdims=True) * inv_n
        delta = alpha - arr[par, :, 1]
        rest = arr[par, :, 2] + delta * (delta * arr[par, :, 4] - 2.0 * arr[par, :, 3])
        beta = jnp.sqrt(jnp.sum(rest, axis=0, keepdims=True) * inv_n)
        alpha_ref[pl.ds(j, 1), :] = alpha
        beta_ref[pl.ds(j, 1), :] = beta
        bsc[0:1, :] = beta
        alpha11 = alpha[:, 0:1]
        beta11 = beta[:, 0:1]

        def update(p, _):
            vs[nxt, p] = (sacc[3, p] - alpha11 * vs[cur, p] - beta_prev * vs[prv, p]) / beta11
            return 0
        lax.fori_loop(0, 16, update, 0)
        out_copy(nxt, j + 1).start()

        @pl.when(j < KRYLOV_STEPS - 1)
        def _():
            for ch in range(NC):
                def fill(pp, _):
                    even = vs[nxt, 2 * pp].astype(bf16)
                    odd = vs[nxt, 2 * pp + 1].astype(bf16)
                    for r in range(4):
                        vsend[r, pp, :, 0:128] = even[:, r * 128:(r + 1) * 128]
                        vsend[r, pp, :, 128:256] = odd[:, r * 128:(r + 1) * 128]
                    vbuf[unit, pp, own_rows, :] = vsend[role, pp]
                    return 0
                lax.fori_loop(ch * ppc, (ch + 1) * ppc, fill, 0)
                for i in range(3):
                    aa_copy(ch, i).start()
        return 0

    lax.fori_loop(0, KRYLOV_STEPS, step, 0)
    out_copy(KRYLOV_STEPS % 3, KRYLOV_STEPS).wait()


def run_kernel(elem_count, vb0, lh, kron, rr, v0):
    f32, bf16 = jnp.float32, jnp.bfloat16
    vm = pl.BlockSpec(memory_space=pltpu.VMEM)
    dma = pltpu.SemaphoreType.DMA
    return pl.pallas_call(
        functools.partial(kernel, elem_count),
        out_shape=(jax.ShapeDtypeStruct((KRYLOV_STEPS + 1, 16, 16, 512), f32),
                   jax.ShapeDtypeStruct((8, 128), f32), jax.ShapeDtypeStruct((8, 128), f32)),
        in_specs=[pl.BlockSpec(memory_space=pl.ANY), vm, vm, vm, pl.BlockSpec(memory_space=pl.ANY)],
        out_specs=(pl.BlockSpec(memory_space=pl.ANY), vm, vm),
        scratch_shapes=[
            pltpu.VMEM((8, 8, 64, 256), bf16),
            pltpu.VMEM((4, 8, 16, 256), bf16),
            pltpu.VMEM((2, NT, 16, 16, 256), bf16),
            pltpu.VMEM((4, 16, 16, 512), f32),
            pltpu.VMEM((3, 16, 16, 512), f32),
            pltpu.VMEM((3, 16, 16, 512), f32),
            pltpu.VMEM((2, NDEV, 8, 128), f32),
            pltpu.VMEM((8, 128), f32),
            dma((2,)), dma, dma((3,)), dma((3,)), dma, dma, dma((NC, 3)), dma((NC, 3)), dma((NC, 7)), dma((NC, 8)),
        ],
        compiler_params=pltpu.CompilerParams(has_side_effects=True, vmem_limit_bytes=67043328),
    )(vb0, lh, kron, rr, v0)


def solution(mesh):

    def index(zh, zl, y, x, c):
        return zh * 16 + zl * 8 + y * 4 + x * 2 + c
    role_groups = [[index(zh, zl, y, x, c) for zl in (0, 1) for x in (0, 1)]
                   for zh in (0, 1) for y in (0, 1) for c in (0, 1)]
    unit_groups = [[index(zh, zl, y, x, c) for zh in (0, 1) for y in (0, 1) for c in (0, 1)]
                   for zl in (0, 1) for x in (0, 1)]

    def local_run(psi_init, left_env, op_pair, right_env):
        f32, bf16 = jnp.float32, jnp.bfloat16
        me = lax.axis_index('terms')
        zh, zl, y, x, c = coords(me)
        role = 2 * zl + x
        elem_count = psi_init.size
        psi = psi_init.reshape(512, 16, 512)
        norm = jnp.sqrt(jnp.sum(psi * psi) / elem_count)
        cols = lax.dynamic_slice_in_dim(psi, role * 128, 128, 2)
        vb0 = (cols / norm).astype(bf16).reshape(2, 2, 2, 2, 2, 16, 8, 2, 128)
        vb0 = vb0.transpose(0, 2, 4, 6, 1, 3, 5, 7, 8).reshape(8, 8, 64, 256)
        v0 = (lax.dynamic_slice_in_dim(psi, me * 16, 16, 0) / norm).transpose(1, 0, 2)

        rr = lax.all_to_all(right_env, 'terms', 1, 0, tiled=True, axis_index_groups=role_groups)
        rr = lax.all_gather(rr, 'terms', axis=0, tiled=True, axis_index_groups=unit_groups)

        lp = left_env.reshape(3, 2, 2, 2, 2, 2, 16, 2, 2, 2, 2, 2, 16)
        lp = lp.transpose(0, 1, 3, 5, 2, 4, 6, 7, 9, 11, 8, 10, 12).reshape(3, 512, 512)
        lp = lax.all_gather(lp, 'terms', axis=0, tiled=True, axis_index_groups=role_groups)
        lp = lax.all_to_all(lp, 'terms', 1, 0, tiled=True, axis_index_groups=unit_groups)
        lh = lp.reshape(NT, 4, 16, 512).transpose(1, 0, 2, 3).reshape(4, NT * 16, 512)

        wk = lax.all_gather(op_pair, 'terms', axis=0, tiled=True).reshape(2, 2, 2, 2, 2, 3, 16, 16)
        wk = wk.transpose(0, 2, 4, 1, 3, 5, 6, 7).reshape(NT, 16, 16)
        eye = jnp.eye(16, dtype=bf16)
        kron = (wk[:, :, None, :, None] * eye[None, None, :, None, :]).reshape(NT, 256, 256)

        out, alpha, beta = run_kernel(elem_count, vb0, lh, kron, rr, v0)
        vecs = out.transpose(0, 2, 1, 3).reshape(KRYLOV_STEPS + 1, 16, 4, 4, 512)
        return vecs, alpha[:KRYLOV_STEPS, 0], beta[:KRYLOV_STEPS, 0]

    return jax.shard_map(local_run, mesh=mesh, in_specs=(P(), P('terms'), P('terms'), P('terms')),
                         out_specs=(P(None, 'terms'), P(), P()), check_vma=False)
```

time: 2770 us -> 1180 us (0.43)
  waiting for transfers between devices: 1550 us -> 138 us
  Pallas kernels: 0 us -> 610 us
  matrix products: 500 us -> 0 us
  blocking collectives: 487 us -> 195 us
    reduce_scatter x6 -> x0, waiting for transfers between devices: 1080 us -> none  [local_run(): lax.psum_scatter(partial_sigma, 'terms', scatter_dimension=0, tiled=True)]
    pallas_call x0 -> x1, Pallas kernels: none -> 610 us  [run_kernel(): pl.pallas_call(functools.partial(kernel, elem_count), out_shape=(jax.Shap...]
    dot_general x18 -> x0, matrix products: 500 us -> none  [the longest x6 254 us: local_run(): jnp.einsum('kax,kxqb->aqb', left_env, z_part, preferred_element_type=jnp....]
    psum x12 -> x0, blocking collectives: 487 us -> none  [the longest x6 255 us: local_run(): alpha_val = lax.psum(jnp.sum(sigma_slab * vector), 'terms') / elem_count]
    all_gather x6 -> x2, waiting for transfers between devices: 470 us -> 68.6 us  [the longest x1 68.6 us: local_run(): lax.all_gather(lp, 'terms', axis=0, tiled=True, axis_index_groups=role_gr...]
    all_gather x0 -> x1, blocking collectives: none -> 135 us  [local_run(): lax.all_gather(op_pair, 'terms', axis=0, tiled=True)]
    dot_general x6 -> x0, local copies, waits for them, and re-layouts: 121 us -> none  [local_run(): jnp.einsum('kax,kxqb->aqb', left_env, z_part, preferred_element_type=jnp....]
    reshape x1 -> x5, local copies, waits for them, and re-layouts: 19.5 us -> 102 us  [the longest x2 63.4 us: local_run(): lp = left_env.reshape(3, 2, 2, 2, 2, 2, 16, 2, 2, 2, 2, 2, 16)]
  transfers between devices with their start and end apart: 12 -> 3, of which waited for: 12 -> 2; matrix products, arithmetic and copies ran while one was open for 0% -> 9% of each run, Pallas kernels for 0% -> 0%
where the time goes in v1:
time: 1180 us; the launch traced here: 1170 us
  Pallas kernels  610 us (52%)
  blocking collectives  195 us (17%)
  local copies, waits for them, and re-layouts  180 us (15%)
  waiting for transfers between devices  138 us (12%)
  other arithmetic  25.9 us (2%)
  between operations  15.3 us (1%)
    pallas_call x1, Pallas kernels, run_kernel(): pl.pallas_call(functools.partial(kernel, elem_count), out_shape=(jax.Shap...  610 us
    all_gather x1, blocking collectives, local_run(): lax.all_gather(op_pair, 'terms', axis=0, tiled=True)  135 us
    all_to_all x1, waiting for transfers between devices, local_run(): lax.all_to_all(lp, 'terms', 1, 0, tiled=True, axis_index_groups=unit_groups)  69.8 us
    all_gather x1, waiting for transfers between devices, local_run(): lax.all_gather(lp, 'terms', axis=0, tiled=True, axis_index_groups=role_gr...  68.6 us
    reshape x2, local copies, waits for them, and re-layouts, local_run(): lp = left_env.reshape(3, 2, 2, 2, 2, 2, 16, 2, 2, 2, 2, 2, 16)  63.4 us
    all_to_all x1, blocking collectives, local_run(): lax.all_to_all(right_env, 'terms', 1, 0, tiled=True, axis_index_groups=ro...  60.4 us
    reshape x1, local copies, waits for them, and re-layouts, local_run(): lp.transpose(0, 1, 3, 5, 2, 4, 6, 7, 9, 11, 8, 10, 12).reshape(3, 512, 512)  35.9 us
    mul x5, local copies, waits for them, and re-layouts, local_run(): wk[:, :, None, :, None] * eye[None, None, :, None, :]  28.2 us
  transfers between devices with their start and end apart: 3, of which 2 were waited for; matrix products, arithmetic and copies ran while one was open for 9% of the time, Pallas kernels for 0%

profile of v1, /device:TPU:0, one launch (start us, length us, event | category | flops | bytes accessed | tf_op | source)
XLA Modules:
  0.0 1169.4 jit_solution(10850190694251479894)
XLA Ops:
  7.2 0.0 all-gather.3.cloned.1.call-start
  7.2 37.7 %reshape.49 = bf16[3,2,2,2,2,2,16,2,2,2,2,2,16]{12,11,10,9,8,7,6,5,4,3,2,1,0:T(2,128)(2,1)} reshape(bf16[3,512,512]{2,1,0:T(8,128)(2,1)} %param.5) | data formatting | bytes 3145728 | tf_op jit(solution)/shard_map/reshape | solution.py:316
  44.9 25.7 %copy.47 = bf16[3,2,2,2,2,2,16,2,2,2,2,2,16]{12,10,8,11,9,7,6,4,2,5,3,1,0:T(2,128)(2,1)} copy(bf16[3,2,2,2,2,2,16,2,2,2,2,2,16]{12,11,10,9,8,7,6,5,4,3,2,1,0:T(2,128)(2,1)} %reshape.49) | data formatting | bytes 3145728 | tf_op jit(solution)/shard_map/reshape | solution.py:316
  70.6 0.0 copy-start
  70.6 35.9 %reshape.50 = bf16[3,512,512]{2,1,0:T(8,128)(2,1)} reshape(bf16[3,2,2,2,2,2,16,2,2,2,2,2,16]{12,11,10,9,8,7,6,5,4,3,2,1,0:T(2,128)(2,1)} %bitcast.31) | data formatting | bytes 3145728 | tf_op jit(solution)/shard_map/reshape | solution.py:317
  106.5 0.0 all-gather.3.cloned.1.call-update
  106.5 0.0 all-gather.5.cloned.1.call-start
  106.6 0.0 copy-done
  106.6 1.4 copy.42
  107.9 60.4 %all_to_all.33 = bf16[3,512,512]{2,0,1:T(4,128)(2,1)S(1)} all-to-all(bf16[3,512,512]{2,0,1:T(4,128)(2,1)S(1)} %copy.42), channel_id=1, replica_groups={{0,2,8,10},{1,3,9,11},{4,6,12,14},{5,7,13,15},{16,18,24,26},{17,19,25,2..., dimensions={1} | all-to-all | bytes 3145728 | tf_op jit(solution)/shard_map/all_to_all | solution.py:313
  168.3 1.6 copy.43
  169.9 0.0 all-gather.5.cloned.1.call-update
  169.9 68.6 %all-gather.3.cloned.1.call-done = bf16[12,512,512]{2,1,0:T(8,128)(2,1)} async-done(((bf16[3,512,512]{2,1,0:T(8,128)(2,1)}), bf16[12,512,512]{2,1,0:T(8,128)(2,1)}) %all-gather.3.cloned.1.call-update) | async-done | bytes 6291472 | tf_op jit(solution)/shard_map/all_gather | solution.py:318
  238.6 9.8 copy.35
  248.4 4.9 all-to-all-start
  253.4 15.8 %copy.32 = f32[512,4,4,512]{3,0,2,1:T(8,128)} copy(f32[512,4,4,512]{3,2,1,0:T(4,128)} %param.4) | data formatting | bytes 33554432 | tf_op args[0]
  269.2 10.9 multiply_reduce_fusion
  280.8 0.0 copy-start.1
  280.8 2.7 divide_convert_fusion
  283.5 3.2 copy.33
  286.7 2.6 reshape.48.vb0_ref
  289.3 0.0 copy-done.1
  289.3 134.7 %all_gather.10 = bf16[96,16,16]{2,1,0:T(8,128)(2,1)S(1)} all-gather(bf16[3,16,16]{2,1,0:T(8,128)(2,1)S(1)} %copy-done.1), channel_id=1, replica_groups=mesh['terms'=32] {'terms'}, dimensions={0}, use_global_device_ids=true | all-gather | bytes 50688 | tf_op jit(solution)/shard_map/all_gather | solution.py:322
  424.1 0.3 copy.40
  424.4 6.3 mul.39
  430.7 20.4 %copy.41 = bf16[96,256,256]{2,1,0:T(8,128)(2,1)} copy(bf16[96,256,256]{0,2,1:T(8,128)(2,1)} %bitcast.30) | data formatting | bytes 25165824 | tf_op jit(solution)/shard_map/mul | solution.py:325
  451.1 0.2 mul.41
  451.3 1.0 mul.42
  452.3 1.9 divide_bitcast_fusion.v0_ref
  454.2 10.5 broadcast_multiply_fusion.kr_ref
  464.7 69.8 %all-to-all-done = bf16[12,512,512]{2,0,1:T(8,128)(2,1)} async-done(((bf16[12,512,512]{2,0,1:T(8,128)(2,1)}), bf16[12,512,512]{2,0,1:T(8,128)(2,1)}, u32[]{:S(2)}, u32[]{:S(2)}) %all-to-all-start) | async-done | bytes 6291488 | tf_op jit(solution)/shard_map/all_to_all | solution.py:319
  534.5 7.2 copy.37
  541.7 3.6 copy.38
  545.3 0.0 all-gather.5.cloned.1.call-done.rr_ref
  545.3 609.9 %shard_map.67 = (f32[7,16,16,512]{3,2,1,0:T(8,128)}, f32[8,128]{1,0:T(8,128)}, f32[8,128]{1,0:T(8,128)}) custom-call(bf16[8,8,64,256]{3,2,1,0:T(8,128)(2,1)} %reshape.48.vb0_ref, bf16[4,1536,512]{2,1,0:T(8,128)(2,1)} %bitcast.34, bf16[96,256,256]{2,1,0:T(8,128)(2,1)} %broadcast_multiply_fusion.kr_ref, ...), custom_call_target="tpu_custom_call" | custom-call | tf_op jit(solution)/shard_map/pallas_call | solution.py:270
  1155.2 0.0 copy-start.2
  1155.2 0.0 copy-start.3
  1155.2 6.3 copy.44
  1161.5 0.0 copy-done.2
  1161.5 0.0 copy-done.3
  1161.5 0.7 slice_reduce_fusion
  (2 shorter events, 0.0 us)
Async XLA Ops:
  7.2 231.4 %all-gather.3.cloned.1.call-start = ((), (), s32[]{:S(2)}) async-start(), calls=%async_computation.2 | async-start | bytes 7864320 | tf_op jit(solution)/shard_map/all_gather | solution.py:318
  70.6 36.0 %copy-start = (bf16[3,512,512]{2,1,0:T(8,128)(2,1)S(1)}, bf16[3,512,512]{2,1,0:T(8,128)(2,1)}, u32[]{:S(2)}) copy-start(bf16[3,512,512]{2,1,0:T(8,128)(2,1)} %param.7) | copy-start | bytes 4718596
  106.5 438.8 %all-gather.5.cloned.1.call-start = ((), (), s32[]{:S(2)}) async-start(), calls=%async_computation.3 | async-start | bytes 14155776 | tf_op jit(solution)/shard_map/all_gather | solution.py:314
  248.4 286.1 %all-to-all-start = ((bf16[12,512,512]{2,0,1:T(8,128)(2,1)}), bf16[12,512,512]{2,0,1:T(8,128)(2,1)}, u32[]{:S(2)}, u32[]{:S(2)}) async-start(bf16[12,512,512]{2,0,1:T(8,128)(2,1)} %copy.35), calls=%async_computation | async-start | bytes 16777216 | tf_op jit(solution)/shard_map/all_to_all | solution.py:319
  280.8 8.5 copy-start.1
  1155.2 6.3 copy-start.2
  1155.2 6.3 copy-start.3
Sparse Core Ops, SparseCore 0:
  106.6 131.8 all-gather.2
  240.4 265.0 all-gather.4

commit v2 on v1

--- a/solution.py
+++ b/solution.py
@@ -12,8 +12,8 @@
 NDEV = 32
 NT = 96
 NC = 4
-GP = 4
-GR = 16
+GP = 16
+GR = 32
 
 
 def coords(me):
@@ -25,9 +25,10 @@
     return zh * 16 + zl * 8 + y * 4 + x * 2 + c
 
 
-def kernel(elem_count, vb0_ref, lh_ref, kr_ref, rr_ref, v0_ref, out_ref, alpha_ref, beta_ref,
-           vbuf, vsend, xs, sacc, rsr, vs, arr, bsc,
-           in_sem, out_sem, rs_send, rs_recv, ar_send, ar_recv, aa_send, aa_recv, ag_send, ag_recv):
+def kernel(elem_count, vb0_ref, left_ref, wx_ref, right_ref, v0_ref, out_ref, alpha_ref, beta_ref,
+           lh_ref, kr_ref, rr_ref, vbuf, vsend, xs, sacc, rsr, vs, arr, bsc,
+           in_sem, w_send, w_recv, r1_send, r1_recv, rg_send, rg_recv, l1_send, l1_recv, l2_send, l2_recv,
+           out_sem, rs_send, rs_recv, ar_send, ar_recv, aa_send, aa_recv, ag_send, ag_recv):
     f32, bf16 = jnp.float32, jnp.bfloat16
     me = lax.axis_index('terms')
     zh, zl, y, x, c = coords(me)
@@ -39,19 +40,19 @@
     dev_z = dev_id(1 - zh, zl, y, x, c)
     dev_y = dev_id(zh, zl, 1 - y, x, c)
     dev_c = dev_id(zh, zl, y, x, 1 - c)
-    own_rows = pl.ds(pl.multiple_of(role * 16, 16), 16)
+    kpos = 4 * unit + role
     ppc = 8 // NC
 
     def aa_copy(ch, i):
         pps = pl.ds(ch * ppc, ppc)
         return pltpu.make_async_remote_copy(
-            src_ref=vsend.at[rs_role[i], pps], dst_ref=vbuf.at[unit, pps, own_rows],
+            src_ref=vsend.at[rs_role[i], pps], dst_ref=vbuf.at[zh, zl, y, x, c, pps],
             send_sem=aa_send.at[ch, i], recv_sem=aa_recv.at[ch, i], device_id=(rs_dev[i],), device_id_type=MESH)
 
     def ag_copy(ch, slot, u, dev):
-        pps = pl.ds(ch * ppc, ppc)
-        return pltpu.make_async_remote_copy(
-            src_ref=vbuf.at[u, pps], dst_ref=vbuf.at[u, pps],
+        block = vbuf.at[u // 4, :, lax.rem(u // 2, 2), :, lax.rem(u, 2), pl.ds(ch * ppc, ppc)]
+        return pltpu.make_async_remote_copy(
+            src_ref=block, dst_ref=block,
             send_sem=ag_send.at[ch, slot], recv_sem=ag_recv.at[ch, u], device_id=(dev,), device_id_type=MESH)
 
     unit_z = 4 * (1 - zh) + 2 * y + c
@@ -87,26 +88,17 @@
             for b in range(2):
                 recv(ch, 4 * a + 2 * b + (1 - c))
 
-    def left_chunk(ch):
-        def body(i, _):
-            pp = ch * ppc + i // 4
-            ac = lax.rem(i, 4)
-            slab = jnp.where(ac == 0, rs_role[0], jnp.where(ac == 1, rs_role[1], jnp.where(ac == 2, rs_role[2], role)))
-            rhs = vbuf[:, pp].reshape(512, 256)
-            res = jnp.dot(lh_ref[slab], rhs, preferred_element_type=f32).astype(bf16).reshape(NT, 16, 256)
-            ap = ac // 2
-
-            @pl.when(lax.rem(ac, 2) == 0)
-            def _():
-                xs[ap, :, 2 * pp, :, 0:128] = res[:, :, 0:128]
-                xs[ap, :, 2 * pp + 1, :, 0:128] = res[:, :, 128:256]
-
-            @pl.when(lax.rem(ac, 2) == 1)
-            def _():
-                xs[ap, :, 2 * pp, :, 128:256] = res[:, :, 0:128]
-                xs[ap, :, 2 * pp + 1, :, 128:256] = res[:, :, 128:256]
-            return 0
-        lax.fori_loop(0, ppc * 4, body, 0)
+    def left_part(pp):
+        def body(ap, _):
+            rhs = vbuf[:, :, :, :, :, pp].reshape(512, 256)
+            for h in range(2):
+                slab = jnp.where(ap == 0, rs_role[h], rs_role[2 + h])
+                res = jnp.dot(lh_ref[slab].reshape(NT * 16, 512), rhs, preferred_element_type=f32)
+                res = res.astype(bf16).reshape(NT, 16, 256)
+                xs[ap, :, 2 * pp, :, h * 128:(h + 1) * 128] = res[:, :, 0:128]
+                xs[ap, :, 2 * pp + 1, :, h * 128:(h + 1) * 128] = res[:, :, 128:256]
+            return 0
+        lax.fori_loop(0, 2, body, 0)
 
     def pair_phase(ap):
         def body(i, _):
@@ -140,11 +132,128 @@
     def out_copy(slot, j):
         return pltpu.make_async_copy(vs.at[slot], out_ref.at[j], out_sem)
 
+    order = [role] + rs_role[:3]
+
+    def r_rows(u, ro):
+        return pl.ds(12 * u + 3 * ro, 3)
+
+    def r1_copy(i):
+        return pltpu.make_async_remote_copy(
+            src_ref=right_ref.at[:, pl.ds(pl.multiple_of(128 * rs_role[i], 128), 128)],
+            dst_ref=rr_ref.at[r_rows(unit, role)],
+            send_sem=r1_send.at[i], recv_sem=r1_recv.at[i], device_id=(rs_dev[i],), device_id_type=MESH)
+
+    def rg_copy(i, slot, u, dev):
+        rows = r_rows(u, order[i])
+        return pltpu.make_async_remote_copy(
+            src_ref=rr_ref.at[rows], dst_ref=rr_ref.at[rows],
+            send_sem=rg_send.at[i, slot], recv_sem=rg_recv.at[i, u], device_id=(dev,), device_id_type=MESH)
+
+    def l_rows(d):
+        return left_ref.at[:, pl.ds(pl.multiple_of(16 * d, 16), 16)]
+
+    def l1_copies(n):
+        uzh, uy, uc = lax.rem(zh + n // 4, 2), lax.rem(y + (n // 2) % 2, 2), lax.rem(c + n % 2, 2)
+        dev = dev_id(uzh, zl, uy, x, uc)
+        return [pltpu.make_async_remote_copy(
+            src_ref=l_rows(dev_id(uzh, r // 2, uy, r % 2, uc)), dst_ref=lh_ref.at[r, unit, role],
+            send_sem=l1_send, recv_sem=l1_recv, device_id=(dev,), device_id_type=MESH) for r in range(4)]
+
+    def l2_copy(i):
+        return pltpu.make_async_remote_copy(
+            src_ref=lh_ref.at[:, :, role], dst_ref=lh_ref.at[:, :, role],
+            send_sem=l2_send.at[i], recv_sem=l2_recv.at[i], device_id=(rs_dev[i],), device_id_type=MESH)
+
+    def w_copy(i):
+        return pltpu.make_async_remote_copy(
+            src_ref=wx_ref, dst_ref=xs.at[1, pl.ds(3 * kpos, 3), 0], send_sem=w_send, recv_sem=w_recv,
+            device_id=(lax.rem(me + i, NDEV),), device_id_type=MESH)
+
+    def local_wait(ref, sem):
+        pltpu.make_async_copy(ref, ref, sem).wait()
+
+    def gather_operators():
+        own_r = pltpu.make_async_copy(
+            right_ref.at[:, pl.ds(pl.multiple_of(128 * role, 128), 128)], rr_ref.at[r_rows(unit, role)], in_sem.at[2])
+        own_w = pltpu.make_async_copy(wx_ref, xs.at[1, pl.ds(3 * kpos, 3), 0], in_sem.at[3])
+        own_l = [pltpu.make_async_copy(l_rows(dev_id(zh, r // 2, y, r % 2, c)), lh_ref.at[r, unit, role],
+                                       in_sem.at[4 + r]) for r in range(4)]
+        own_r.start()
+        own_w.start()
+        for cp in own_l:
+            cp.start()
+        for i in range(3):
+            r1_copy(i).start()
+        for n in range(1, 8):
+            for cp in l1_copies(n):
+                cp.start()
+
+        def send_w(i, _):
+            w_copy(i).start()
+            return 0
+        lax.fori_loop(1, NDEV, send_w, 0)
+
+        def r_start(i, slots):
+            for k in slots:
+                rg_copy(i, *sends[k]).start()
+
+        def r_recv(i, u):
+            rg_copy(i, 0, u, dev_c).wait_recv()
+
+        own_r.wait()
+        r_start(0, (0, 1, 3))
+        for i in range(3):
+            r1_copy(i).wait_recv()
+            r_start(i + 1, (0, 1, 3))
+        for cp in own_l:
+            cp.wait()
+        l1_part = lh_ref.at[:, pl.ds(0, 7), 0]
+        local_wait(l1_part, l1_recv)
+        for i in range(3):
+            l2_copy(i).start()
+
+        own_w.wait()
+        w_part = xs.at[1, pl.ds(0, 93), 0]
+        local_wait(w_part, w_recv)
+        keep = lax.rem(lax.broadcasted_iota(jnp.int32, (16, 256), 1), 16) == lax.broadcasted_iota(jnp.int32, (16, 256), 0)
+
+        def build(k, _):
+            w = xs[1, k, 0].astype(f32)
+            for q in range(16):
+                kr_ref[k, q * 16:(q + 1) * 16, :] = jnp.where(keep, w[q:q + 1, :], 0.0).astype(bf16)
+            return 0
+        lax.fori_loop(0, NT, build, 0)
+
+        for t in range(5):
+            if t < 4:
+                r_recv(t, unit_z)
+                r_start(t, (2, 4))
+                r_recv(t, unit_y)
+                r_start(t, (5,))
+            if t >= 1:
+                r_recv(t - 1, unit_zy)
+                r_start(t - 1, (6,))
+        for i in range(3):
+            l2_copy(i).wait_recv()
+        for i in range(4):
+            for a in range(2):
+                for b in range(2):
+                    r_recv(i, 4 * a + 2 * b + (1 - c))
+        for i in range(3):
+            r1_copy(i).wait_send()
+            l2_copy(i).wait_send()
+        local_wait(l1_part, l1_send)
+        local_wait(w_part, w_send)
+        for i in range(4):
+            for k in sends:
+                rg_copy(i, *k).wait_send()
+
     loads = [pltpu.make_async_copy(v0_ref, vs.at[0], in_sem.at[0]), pltpu.make_async_copy(vb0_ref, vbuf, in_sem.at[1])]
     for cp in loads:
         cp.start()
     vs[2] = jnp.zeros((16, 16, 512), f32)
     bsc[...] = jnp.zeros((8, 128), f32)
+    gather_operators()
     for cp in loads:
         cp.wait()
     out_copy(0, 0).start()
@@ -155,21 +264,27 @@
         prv = lax.rem(j + 2, 3)
         par = lax.rem(j, 2)
 
-        @pl.when(j > 0)
-        def _():
-            for t in range(NC + 2):
-                if t < NC:
-                    stage_a(t)
-                if 0 <= t - 1 < NC:
-                    stage_z(t - 1)
-                if 0 <= t - 2 < NC:
-                    stage_y(t - 2)
-
-        for ch in range(NC):
+        def arrivals(*stages):
             @pl.when(j > 0)
             def _():
-                stage_c(ch)
-            left_chunk(ch)
+                for stage, ch in stages:
+                    stage(ch)
+
+        arrivals((stage_a, 0), (stage_a, 1), (stage_a, 2), (stage_a, 3),
+                 (stage_z, 0), (stage_z, 1), (stage_y, 0), (stage_c, 0))
+        left_part(0)
+        arrivals((stage_z, 2), (stage_y, 1))
+        left_part(1)
+        arrivals((stage_z, 3), (stage_y, 2), (stage_c, 1))
+        left_part(2)
+        arrivals((stage_y, 3), )
+        left_part(3)
+        arrivals((stage_c, 2), )
+        left_part(4)
+        left_part(5)
+        arrivals((stage_c, 3), )
+        left_part(6)
+        left_part(7)
 
         @pl.when(j > 0)
         def _():
@@ -252,7 +367,7 @@
                     for r in range(4):
                         vsend[r, pp, :, 0:128] = even[:, r * 128:(r + 1) * 128]
                         vsend[r, pp, :, 128:256] = odd[:, r * 128:(r + 1) * 128]
-                    vbuf[unit, pp, own_rows, :] = vsend[role, pp]
+                    vbuf[zh, zl, y, x, c, pp] = vsend[role, pp]
                     return 0
                 lax.fori_loop(ch * ppc, (ch + 1) * ppc, fill, 0)
                 for i in range(3):
@@ -263,18 +378,22 @@
     out_copy(KRYLOV_STEPS % 3, KRYLOV_STEPS).wait()
 
 
-def run_kernel(elem_count, vb0, lh, kron, rr, v0):
+def run_kernel(elem_count, vb0, left, wx, right, v0):
     f32, bf16 = jnp.float32, jnp.bfloat16
     vm = pl.BlockSpec(memory_space=pltpu.VMEM)
+    anyspace = pl.BlockSpec(memory_space=pl.ANY)
     dma = pltpu.SemaphoreType.DMA
     return pl.pallas_call(
         functools.partial(kernel, elem_count),
         out_shape=(jax.ShapeDtypeStruct((KRYLOV_STEPS + 1, 16, 16, 512), f32),
                    jax.ShapeDtypeStruct((8, 128), f32), jax.ShapeDtypeStruct((8, 128), f32)),
-        in_specs=[pl.BlockSpec(memory_space=pl.ANY), vm, vm, vm, pl.BlockSpec(memory_space=pl.ANY)],
-        out_specs=(pl.BlockSpec(memory_space=pl.ANY), vm, vm),
+        in_specs=[anyspace] * 5,
+        out_specs=(anyspace, vm, vm),
         scratch_shapes=[
-            pltpu.VMEM((8, 8, 64, 256), bf16),
+            pltpu.VMEM((4, 8, 4, 3, 16, 512), bf16),
+            pltpu.VMEM((NT, 256, 256), bf16),
+            pltpu.VMEM((NT, 128, 512), bf16),
+            pltpu.VMEM((2, 2, 2, 2, 2, 8, 16, 256), bf16),
             pltpu.VMEM((4, 8, 16, 256), bf16),
             pltpu.VMEM((2, NT, 16, 16, 256), bf16),
             pltpu.VMEM((4, 16, 16, 512), f32),
@@ -282,49 +401,28 @@
             pltpu.VMEM((3, 16, 16, 512), f32),
             pltpu.VMEM((2, NDEV, 8, 128), f32),
             pltpu.VMEM((8, 128), f32),
-            dma((2,)), dma, dma((3,)), dma((3,)), dma, dma, dma((NC, 3)), dma((NC, 3)), dma((NC, 7)), dma((NC, 8)),
+            dma((8,)), dma, dma, dma((3,)), dma((3,)), dma((4, 7)), dma((4, 8)), dma, dma, dma((3,)), dma((3,)),
+            dma, dma((3,)), dma((3,)), dma, dma, dma((NC, 3)), dma((NC, 3)), dma((NC, 7)), dma((NC, 8)),
         ],
         compiler_params=pltpu.CompilerParams(has_side_effects=True, vmem_limit_bytes=67043328),
-    )(vb0, lh, kron, rr, v0)
+    )(vb0, left, wx, right, v0)
 
 
 def solution(mesh):
-
-    def index(zh, zl, y, x, c):
-        return zh * 16 + zl * 8 + y * 4 + x * 2 + c
-    role_groups = [[index(zh, zl, y, x, c) for zl in (0, 1) for x in (0, 1)]
-                   for zh in (0, 1) for y in (0, 1) for c in (0, 1)]
-    unit_groups = [[index(zh, zl, y, x, c) for zh in (0, 1) for y in (0, 1) for c in (0, 1)]
-                   for zl in (0, 1) for x in (0, 1)]
-
     def local_run(psi_init, left_env, op_pair, right_env):
         f32, bf16 = jnp.float32, jnp.bfloat16
         me = lax.axis_index('terms')
         zh, zl, y, x, c = coords(me)
         role = 2 * zl + x
         elem_count = psi_init.size
-        psi = psi_init.reshape(512, 16, 512)
-        norm = jnp.sqrt(jnp.sum(psi * psi) / elem_count)
-        cols = lax.dynamic_slice_in_dim(psi, role * 128, 128, 2)
-        vb0 = (cols / norm).astype(bf16).reshape(2, 2, 2, 2, 2, 16, 8, 2, 128)
-        vb0 = vb0.transpose(0, 2, 4, 6, 1, 3, 5, 7, 8).reshape(8, 8, 64, 256)
-        v0 = (lax.dynamic_slice_in_dim(psi, me * 16, 16, 0) / norm).transpose(1, 0, 2)
-
-        rr = lax.all_to_all(right_env, 'terms', 1, 0, tiled=True, axis_index_groups=role_groups)
-        rr = lax.all_gather(rr, 'terms', axis=0, tiled=True, axis_index_groups=unit_groups)
-
-        lp = left_env.reshape(3, 2, 2, 2, 2, 2, 16, 2, 2, 2, 2, 2, 16)
-        lp = lp.transpose(0, 1, 3, 5, 2, 4, 6, 7, 9, 11, 8, 10, 12).reshape(3, 512, 512)
-        lp = lax.all_gather(lp, 'terms', axis=0, tiled=True, axis_index_groups=role_groups)
-        lp = lax.all_to_all(lp, 'terms', 1, 0, tiled=True, axis_index_groups=unit_groups)
-        lh = lp.reshape(NT, 4, 16, 512).transpose(1, 0, 2, 3).reshape(4, NT * 16, 512)
-
-        wk = lax.all_gather(op_pair, 'terms', axis=0, tiled=True).reshape(2, 2, 2, 2, 2, 3, 16, 16)
-        wk = wk.transpose(0, 2, 4, 1, 3, 5, 6, 7).reshape(NT, 16, 16)
-        eye = jnp.eye(16, dtype=bf16)
-        kron = (wk[:, :, None, :, None] * eye[None, None, :, None, :]).reshape(NT, 256, 256)
-
-        out, alpha, beta = run_kernel(elem_count, vb0, lh, kron, rr, v0)
+        norm = jnp.sqrt(jnp.sum(psi_init * psi_init) / elem_count)
+        cols = lax.dynamic_slice_in_dim(psi_init, role * 128, 128, 3)
+        vb0 = (cols / norm).astype(bf16).reshape(32, 16, 8, 2, 128)
+        vb0 = vb0.transpose(0, 2, 1, 3, 4).reshape(2, 2, 2, 2, 2, 8, 16, 256)
+        rows = lax.dynamic_slice_in_dim(psi_init, me * 16, 16, 0)
+        v0 = (rows / norm).reshape(16, 16, 512).transpose(1, 0, 2)
+        wx = jnp.broadcast_to(op_pair[:, :, :, None], (3, 16, 16, 16)).reshape(3, 16, 256)
+        out, alpha, beta = run_kernel(elem_count, vb0, left_env, wx, right_env, v0)
         vecs = out.transpose(0, 2, 1, 3).reshape(KRYLOV_STEPS + 1, 16, 4, 4, 512)
         return vecs, alpha[:KRYLOV_STEPS, 0], beta[:KRYLOV_STEPS, 0]
 

time: 1180 us -> 641 us (0.54)
  blocking collectives: 195 us -> 0 us
  local copies, waits for them, and re-layouts: 180 us -> 14 us
  waiting for transfers between devices: 138 us -> 0 us
  between operations: 15.3 us -> 1.41 us
    all_gather x1 -> x0, blocking collectives: 135 us -> none  [local_run(): lax.all_gather(op_pair, 'terms', axis=0, tiled=True)]
    reshape x5 -> x3, local copies, waits for them, and re-layouts: 102 us -> 5.12 us  [the longest x1 2.61 us: local_run(): vb0 = vb0.transpose(0, 2, 1, 3, 4).reshape(2, 2, 2, 2, 2, 8, 16, 256)]
    all_to_all x1 -> x0, waiting for transfers between devices: 69.8 us -> none  [local_run(): lax.all_to_all(lp, 'terms', 1, 0, tiled=True, axis_index_groups=unit_groups)]
    all_gather x2 -> x0, waiting for transfers between devices: 68.6 us -> none  [the longest x1 68.6 us: local_run(): lax.all_gather(lp, 'terms', axis=0, tiled=True, axis_index_groups=role_gr...]
    all_to_all x1 -> x0, blocking collectives: 60.4 us -> none  [local_run(): lax.all_to_all(right_env, 'terms', 1, 0, tiled=True, axis_index_groups=ro...]
    mul x5 -> x0, local copies, waits for them, and re-layouts: 28.2 us -> none  [local_run(): wk[:, :, None, :, None] * eye[None, None, :, None, :]]
    unnamed x11 -> x3, local copies, waits for them, and re-layouts: 23.5 us -> 6.26 us
  transfers between devices with their start and end apart: 3 -> 0, of which waited for: 2 -> 0; matrix products, arithmetic and copies ran while one was open for 9% -> 0% of each run, Pallas kernels for 0% -> 0%
where the time goes in v2:
time: 641 us; the launch traced here: 640 us
  Pallas kernels  610 us (95%)
  other arithmetic  14.9 us (2%)
  local copies, waits for them, and re-layouts  14 us (2%)
    pallas_call x1, Pallas kernels, run_kernel(): pl.pallas_call(functools.partial(kernel, elem_count), out_shape=(jax.Shap...  610 us

profile of v2, /device:TPU:0, one launch (start us, length us, event | category | flops | bytes accessed | tf_op | source)
XLA Modules:
  0.0 640.4 jit_solution(9736806173120077716)
XLA Ops:
  0.7 10.9 %multiply_reduce_fusion = f32[]{:T(128)} fusion(f32[512,4,4,512]{3,2,1,0:T(4,128)} %param.4), kind=kLoop, calls=%fused_computation | loop fusion | flops 8388607 | bytes 16777220 | tf_op jit(solution)/shard_map/reduce_sum | solution.py:418
  12.2 2.9 fusion
  15.2 1.7 copy.14
  16.9 0.0 copy-start
  16.9 2.6 reshape.23.vb0_ref
  19.5 1.2 dynamic-slice_divide_fusion.1
  20.7 1.1 copy.11
  21.8 0.0 copy-done
  21.8 0.2 broadcast_in_dim.2
  22.0 0.8 reshape.24.wx_ref
  22.8 610.0 %shard_map.67 = (f32[7,16,16,512]{3,2,1,0:T(8,128)}, f32[8,128]{1,0:T(8,128)}, f32[8,128]{1,0:T(8,128)}) custom-call(bf16[2,2,2,2,2,8,16,256]{7,6,5,4,3,2,1,0:T(8,128)(2,1)} %reshape.23.vb0_ref, bf16[3,512,512]{2,1,0:T(8,128)(2,1)} %left_ref.1, bf16[3,16,256]{2,1,0:T(8,128)(2,1)} %reshape.24.wx_ref, bf16[3,512,512]{2,1,0:T(8,128)(2,1)} %right_ref.1, ...), custom_call_target="tpu_custom_call" | custom-call | tf_op jit(solution)/shard_map/pallas_call | solution.py:386
  632.8 1.3 slice_reduce_fusion
  634.2 6.3 copy.12
Async XLA Ops:
  16.9 4.9 copy-start

commit v3 on v2

--- a/solution.py
+++ b/solution.py
@@ -11,7 +11,7 @@
 MESH = pl.DeviceIdType.MESH
 NDEV = 32
 NT = 96
-NC = 4
+NC = 8
 GP = 16
 GR = 32
 
@@ -92,7 +92,7 @@
         def body(ap, _):
             rhs = vbuf[:, :, :, :, :, pp].reshape(512, 256)
             for h in range(2):
-                slab = jnp.where(ap == 0, rs_role[h], rs_role[2 + h])
+                slab = jnp.where(ap == 0, rs_role[(2, 0)[h]], rs_role[(1, 3)[h]])
                 res = jnp.dot(lh_ref[slab].reshape(NT * 16, 512), rhs, preferred_element_type=f32)
                 res = res.astype(bf16).reshape(NT, 16, 256)
                 xs[ap, :, 2 * pp, :, h * 128:(h + 1) * 128] = res[:, :, 0:128]
@@ -270,21 +270,12 @@
                 for stage, ch in stages:
                     stage(ch)
 
-        arrivals((stage_a, 0), (stage_a, 1), (stage_a, 2), (stage_a, 3),
-                 (stage_z, 0), (stage_z, 1), (stage_y, 0), (stage_c, 0))
-        left_part(0)
-        arrivals((stage_z, 2), (stage_y, 1))
-        left_part(1)
-        arrivals((stage_z, 3), (stage_y, 2), (stage_c, 1))
-        left_part(2)
-        arrivals((stage_y, 3), )
-        left_part(3)
-        arrivals((stage_c, 2), )
-        left_part(4)
-        left_part(5)
-        arrivals((stage_c, 3), )
-        left_part(6)
-        left_part(7)
+        arrivals(*[(stage_a, ch) for ch in range(NC)], (stage_z, 0), (stage_z, 1), (stage_y, 0))
+        for ch in range(NC):
+            later = [(stage_z, ch + 2)] if ch + 2 < NC else []
+            later += [(stage_y, ch + 1)] if ch + 1 < NC else []
+            arrivals(*later, (stage_c, ch))
+            left_part(ch)
 
         @pl.when(j > 0)
         def _():
@@ -295,13 +286,13 @@
                     ag_copy(ch, *s).wait_send()
 
         pair_phase(0)
-        right_phase(0, 0, 0)
+        right_phase(0, 0, 2)
+        rs_copy(2).start()
+        right_phase(0, 1, 0)
         rs_copy(0).start()
-        right_phase(0, 1, 1)
+        pair_phase(1)
+        right_phase(1, 0, 1)
         rs_copy(1).start()
-        pair_phase(1)
-        right_phase(1, 0, 2)
-        rs_copy(2).start()
         right_phase(1, 1, 3)
         out_copy(cur, j).wait()
         for i in range(3):

time: 641 us -> 618 us (0.964)
  Pallas kernels: 610 us -> 587 us
    pallas_call x1, Pallas kernels: 610 us -> 587 us  [run_kernel(): pl.pallas_call(functools.partial(kernel, elem_count), out_shape=(jax.Shap...]
where the time goes in v3:
time: 618 us
  Pallas kernels  587 us (95%)
  other arithmetic  14.9 us (2%)
  local copies, waits for them, and re-layouts  14 us (2%)
    pallas_call x1, Pallas kernels, run_kernel(): pl.pallas_call(functools.partial(kernel, elem_count), out_shape=(jax.Shap...  587 us

profile of v3, /device:TPU:0, one launch (start us, length us, event | category | flops | bytes accessed | tf_op | source)
XLA Modules:
  0.0 617.6 jit_solution(10926258708487664315)
XLA Ops:
  0.7 10.9 %multiply_reduce_fusion = f32[]{:T(128)} fusion(f32[512,4,4,512]{3,2,1,0:T(4,128)} %param.4), kind=kLoop, calls=%fused_computation | loop fusion | flops 8388607 | bytes 16777220 | tf_op jit(solution)/shard_map/reduce_sum | solution.py:409
  12.2 2.9 fusion
  15.2 1.7 copy.14
  16.9 0.0 copy-start
  16.9 2.6 reshape.23.vb0_ref
  19.5 1.2 dynamic-slice_divide_fusion.1
  20.7 1.1 copy.11
  21.8 0.0 copy-done
  21.8 0.2 broadcast_in_dim.2
  22.0 0.8 reshape.24.wx_ref
  22.8 587.2 %shard_map.67 = (f32[7,16,16,512]{3,2,1,0:T(8,128)}, f32[8,128]{1,0:T(8,128)}, f32[8,128]{1,0:T(8,128)}) custom-call(bf16[2,2,2,2,2,8,16,256]{7,6,5,4,3,2,1,0:T(8,128)(2,1)} %reshape.23.vb0_ref, bf16[3,512,512]{2,1,0:T(8,128)(2,1)} %left_ref.1, bf16[3,16,256]{2,1,0:T(8,128)(2,1)} %reshape.24.wx_ref, bf16[3,512,512]{2,1,0:T(8,128)(2,1)} %right_ref.1, ...), custom_call_target="tpu_custom_call" | custom-call | tf_op jit(solution)/shard_map/pallas_call | solution.py:377
  610.0 1.3 slice_reduce_fusion
  611.3 6.3 %copy.12 = f32[7,16,4,4,512]{4,3,2,1,0:T(4,128)} copy(f32[7,16,4,4,512]{4,1,3,2,0:T(8,128)} %bitcast.14) | data formatting | bytes 7340032
Async XLA Ops:
  16.9 4.9 copy-start
